TPU v7x, 32 devices: a whole 2x2x4 slice. The times are simulated.
32 devices in a mesh: lat: 4 (over x, core), lon: 8 (over z, y).
Axes of the slice: x: 2, y: 2, z: 4, core: 2. Of those that a mesh axis runs over, the one named last changes fastest.
Arguments:
- prediction_fields: float32 [4, 69, 360, 512], P(None, None, 'lon', 'lat'), may hold values from -16 to 16
- verifying_state: float32 [69, 360, 512], P(None, 'lon', 'lat'), may hold values from -16 to 16
- normal_state: float32 [69, 360, 512], P(None, 'lon', 'lat'), may hold values from -16 to 16
- evaluated_point_flag: int32 [360, 512], P('lon', 'lat'), may hold values 0 or 1
- parallels_each_strip: int32 [4], replicated, may hold values from 1 to 128, 361 in all
Outputs:
- parallel_quadratic_error: float32 [4, 69, 512], P(None, None, 'lat')
- parallel_systematic_error: float32 [4, 69, 512], P(None, None, 'lat')
- parallel_pattern_skill: float32 [4, 69, 512], P(None, None, 'lat')
- rmse: float32 [4, 69], replicated
- systematic_error: float32 [4, 69], replicated
- pattern_skill: float32 [4, 69], replicated
Inputs may be any that keep to these rules, and one draw needn't show every extreme that they name: `parallels_each_strip`: they sum to 361, and some band holds exactly 128 rows.
All inputs are finite; a program needn't handle non-finite values.
Results may differ from a plain program's by a relative error of at most 0.00002.
Values sent between devices are 32-bit elements.
A program may use at most 64 MiB of HBM per device.

v0:
```python
import jax
import jax.numpy as jnp
from jax import lax
from jax.sharding import PartitionSpec as P

MEAN_ROWS = 90
minimum_divisor = 0.1


def stacked_metrics(totals, horizon_tally, quantity_tally, grid_point_tally):
    block_rows = horizon_tally * quantity_tally
    width = totals.shape[1]
    error_power_two = (
        totals[:block_rows].reshape(horizon_tally, quantity_tally, width) / grid_point_tally
    )
    prediction_error = (
        totals[block_rows : 2 * block_rows].reshape(horizon_tally, quantity_tally, width)
        / grid_point_tally
    )
    paired_anomaly_term = (
        totals[2 * block_rows : 3 * block_rows].reshape(horizon_tally, quantity_tally, width)
        / grid_point_tally
    )
    predicted_spread_sum = (
        totals[3 * block_rows : 4 * block_rows].reshape(horizon_tally, quantity_tally, width)
        / grid_point_tally
    )
    observed_dispersion = (
        totals[4 * block_rows :].reshape(1, quantity_tally, width) / grid_point_tally
    )
    divisor_term = jnp.sqrt(
        jnp.maximum(predicted_spread_sum, minimum_divisor)
        * jnp.maximum(observed_dispersion, minimum_divisor)
    )
    return (error_power_two, prediction_error, paired_anomaly_term / divisor_term)


def local(
    prediction_fields, verifying_state, normal_state, evaluated_point_flag, parallels_each_strip
):
    horizon_tally, quantity_tally, zonal_circle_size, parallel_index = prediction_fields.shape
    lat_bands = lax.axis_size("lat")
    lon_spokes = lax.axis_size("lon")
    lat_total = MEAN_ROWS * lat_bands + 1
    lon_total = zonal_circle_size * lon_spokes
    band_index = lax.axis_index("lat")
    band_ids = jnp.arange(lat_bands, dtype=jnp.int32)
    first_row = jnp.sum(jnp.where(band_ids < band_index, parallels_each_strip, 0))
    band_filled = jnp.sum(jnp.where(band_ids == band_index, parallels_each_strip, 0))
    slot_ids = jnp.arange(parallel_index, dtype=jnp.int32)
    inside_band = slot_ids < band_filled
    angles = jnp.pi * jnp.arange(lat_total, dtype=jnp.float32) / (lat_total - 1)
    normalizer = jnp.sum(jnp.sin(angles))
    row_angle = jnp.pi * (first_row + slot_ids).astype(jnp.float32) / (lat_total - 1)
    area_factors = jnp.where(inside_band, jnp.sin(row_angle) * lat_total / normalizer, 0.0)
    retain_filter = (
        evaluated_point_flag.astype(jnp.float32) * inside_band.astype(jnp.float32)[None, :]
    )
    observed_anomaly = verifying_state - normal_state
    predicted_anomaly = prediction_fields - normal_state[None]
    mistake_field = predicted_anomaly - observed_anomaly[None]
    retained_entries = retain_filter[None, None]
    block_rows = horizon_tally * quantity_tally
    partial_value = jnp.concatenate(
        [
            jnp.sum(retained_entries * mistake_field * mistake_field, axis=2).reshape(
                block_rows, parallel_index
            ),
            jnp.sum(retained_entries * mistake_field, axis=2).reshape(block_rows, parallel_index),
            jnp.sum(retained_entries * predicted_anomaly * observed_anomaly[None], axis=2).reshape(
                block_rows, parallel_index
            ),
            jnp.sum(retained_entries * predicted_anomaly * predicted_anomaly, axis=2).reshape(
                block_rows, parallel_index
            ),
            jnp.sum(retain_filter[None] * observed_anomaly * observed_anomaly, axis=1),
        ],
        axis=0,
    )
    grand = lax.psum(jnp.sum(partial_value * area_factors, axis=1), ("lat", "lon"))
    zonal = lax.psum(partial_value, "lon")
    error_power_two, prediction_error, covariance_sum = stacked_metrics(
        zonal, horizon_tally, quantity_tally, float(lon_total)
    )
    total_square, total_offset, total_agree = stacked_metrics(
        grand[:, None], horizon_tally, quantity_tally, float(lat_total * lon_total)
    )
    rmse = jnp.sqrt(jnp.maximum(total_square[:, :, 0], minimum_divisor))
    return (
        error_power_two,
        prediction_error,
        covariance_sum,
        rmse,
        total_offset[:, :, 0],
        total_agree[:, :, 0],
    )


def solution(mesh):
    in_specs = (
        P(None, None, "lon", "lat"),
        P(None, "lon", "lat"),
        P(None, "lon", "lat"),
        P("lon", "lat"),
        P(),
    )
    out_specs = (P(None, None, "lat"), P(None, None, "lat"), P(None, None, "lat"), P(), P(), P())
    return jax.shard_map(local, mesh=mesh, in_specs=in_specs, out_specs=out_specs, check_vma=False)
```

profile of v0, /device:TPU:0, one launch (start us, length us, event | category | flops | bytes accessed | tf_op | source)
XLA Modules:
  0.0 119.7 jit_solution(12313264060658802673)
XLA Ops:
  7.2 0.0 copy-start.4
  7.2 0.6 sine_reduce_fusion
  7.8 1.3 %fusion.10 = (s32[]{:T(128)}, s32[]{:T(128)}) fusion(s32[4]{0:T(128)} %param.9, s32[]{:T(128)S(6)} %axis_index.15), kind=kLoop, calls=%fused_computation.33 | loop fusion | flops 22 | bytes 28 | tf_op jit(solution)/shard_map/reduce_sum | solution.py:48
  9.1 0.6 compare_convert_fusion
  9.8 0.0 copy-start
  9.8 0.0 copy-start.3
  9.8 1.9 %copy.18 = f32[69,45,128]{2,1,0:T(8,128)S(1)} copy(f32[69,45,128]{2,0,1:T(8,128)} %param.7) | data formatting | bytes 3179520 | tf_op args[2]
  11.7 0.0 copy-done.4
  11.7 0.0 copy-done
  11.8 0.5 copy-done.3
  12.2 0.0 copy-start.1
  12.2 0.3 fusion.3
  12.5 0.3 copy.19
  12.9 2.1 %copy-done.1 = f32[4,69,45,128]{3,0,2,1:T(4,128)S(1)} copy-done((f32[4,69,45,128]{3,0,2,1:T(4,128)S(1)}, f32[4,69,45,128]{3,0,2,1:T(4,128)}, u32[]{:S(2)}) %copy-start.1) | copy-done | bytes 6359064
  15.0 10.1 %fusion.1 = (f32[4,69,128]{2,0,1:T(4,128)S(1)}, f32[4,69,128]{2,0,1:T(4,128)S(1)}, f32[4,69,128]{2,0,1:T(4,128)S(1)}, f32[4,69,128]{2,0,1:T(4,128)S(1)}) fusion(f32[4,69,45,128]{3,0,2,1:T(4,128)S(1)} %copy-done.1, f32[69,45,128]{2,1,0:T(8,128)S(1)} %copy.19, f32[69,45,128]{2,1,0:T(8,128)S(1)} %copy.18, f32[45,128]{1,0:T(8,128)S(1)} %convert_multiply_fusion), kind=kLoop, calls=%fused_computation.5 | loop fusion | flops 17346048 | bytes 10126848 | tf_op jit(solution)/shard_map/reduce_sum | solution.py:70
  25.3 2.0 %compare_select_fusion.2 = f32[128]{0:T(128)S(1)} fusion(f32[]{:T(128)} %sine_reduce_fusion, s32[]{:T(128)} %get-tuple-element.22, s32[]{:T(128)} %get-tuple-element.23), kind=kLoop, calls=%fused_computation.30 | loop fusion | flops 896 | bytes 524 | tf_op jit(solution)/shard_map/jit(_where)/select_n | solution.py:55
  27.3 0.7 concatenate.3
  27.9 0.0 copy-start.2
  27.9 0.2 multiply_reduce_fusion.1
  28.2 0.0 all-reduce.2.cloned.1.call-start
  28.2 0.5 copy-done.2
  28.7 0.2 all-reduce.2.cloned.1.call-update
  28.9 42.2 %psum.15 = f32[1173]{0:T(1024)S(1)} all-reduce(f32[1173]{0:T(1024)S(1)} %multiply_reduce_fusion.1), channel_id=1, replica_groups=mesh['lat'=4,'lon'=8] {'lat','lon'}, use_global_device_ids=true, to_apply=%region_10.11 | all-reduce | flops 1173 | bytes 9384 | tf_op jit(solution)/shard_map/psum | solution.py:80
  71.1 0.1 fusion.6
  71.2 0.1 div.94
  71.3 0.1 max.48
  71.4 0.7 div.92
  72.0 0.7 sqrt.14
  72.7 0.1 fusion.11
  72.8 0.6 rsqrt_multiply_fusion.1
  73.4 35.3 %all-reduce.2.cloned.1.call-done = f32[1173,128]{1,0:T(8,128)} async-done(((f32[1173,128]{1,0:T(8,128)}), f32[1173,128]{1,0:T(8,128)}) %all-reduce.2.cloned.1.call-update) | async-done | bytes 600592 | tf_op jit(solution)/shard_map/psum | solution.py:81
  108.7 1.2 fusion.4
  109.9 0.8 fusion.5
  110.7 0.7 copy.26
  111.4 0.7 copy.24
  112.1 0.7 copy.25
  (14 shorter events, 0.2 us)
Async XLA Ops:
  7.2 4.6 %copy-start.4 = (s32[45,128]{1,0:T(8,128)S(1)}, s32[45,128]{1,0:T(8,128)}, u32[]{:S(2)}) copy-start(s32[45,128]{1,0:T(8,128)} %param.8) | copy-start | bytes 69124
  9.8 2.0 %copy-start = (f32[69,45,128]{2,0,1:T(8,128)S(1)}, f32[69,45,128]{2,0,1:T(8,128)}, u32[]{:S(2)}) copy-start(f32[69,45,128]{2,0,1:T(8,128)} %param.7) | copy-start | bytes 4769284
  9.8 2.4 %copy-start.3 = (f32[69,45,128]{2,0,1:T(8,128)S(1)}, f32[69,45,128]{2,0,1:T(8,128)}, u32[]{:S(2)}) copy-start(f32[69,45,128]{2,0,1:T(8,128)} %param.6) | copy-start | bytes 4769284
  12.2 2.8 %copy-start.1 = (f32[4,69,45,128]{3,0,2,1:T(4,128)S(1)}, f32[4,69,45,128]{3,0,2,1:T(4,128)}, u32[]{:S(2)}) copy-start(f32[4,69,45,128]{3,0,2,1:T(4,128)} %param.5) | copy-start | bytes 19077124
  27.9 0.8 copy-start.2
  28.2 80.5 %all-reduce.2.cloned.1.call-start = ((), (), s32[]{:S(2)}) async-start(), calls=%async_computation | async-start | bytes 1204224 | tf_op jit(solution)/shard_map/psum | solution.py:81
Sparse Core Ops, SparseCore 0:
  32.4 76.1 all-reduce.1
where the time goes:
time: 120 us
  blocking collectives  42.2 us (35%)
  waiting for transfers between devices  35.5 us (30%)
  other arithmetic  18 us (15%)
  between operations  14.2 us (12%)
  local copies, waits for them, and re-layouts  9.77 us (8%)
    psum x1, blocking collectives, local(): lax.psum(jnp.sum(partial_value * area_factors, axis=1), ('lat', 'lon'))  42.2 us
    psum x1, waiting for transfers between devices, local(): zonal = lax.psum(partial_value, 'lon')  35.3 us
    reduce_sum x1, other arithmetic, local(): jnp.sum(retained_entries * predicted_anomaly * observed_anomaly[None], ax...  10.1 us
    unnamed x14, local copies, waits for them, and re-layouts  7.14 us
  transfers between devices with their start and end apart: 1, of which 1 were waited for; matrix products, arithmetic and copies ran while one was open for 2% of the time, Pallas kernels for 0%

commit v1 on v0

--- a/solution.py
+++ b/solution.py
@@ -38,6 +38,10 @@
 def local(
     prediction_fields, verifying_state, normal_state, evaluated_point_flag, parallels_each_strip
 ):
+
+    def match_stacks_all_on_mesh(incoming_x, a_name):
+        return jnp.sum(jax.lax.all_gather(incoming_x, a_name), axis=0)
+
     horizon_tally, quantity_tally, zonal_circle_size, parallel_index = prediction_fields.shape
     lat_bands = lax.axis_size("lat")
     lon_spokes = lax.axis_size("lon")
@@ -78,7 +82,7 @@
         axis=0,
     )
     grand = lax.psum(jnp.sum(partial_value * area_factors, axis=1), ("lat", "lon"))
-    zonal = lax.psum(partial_value, "lon")
+    zonal = match_stacks_all_on_mesh(partial_value, "lon")
     error_power_two, prediction_error, covariance_sum = stacked_metrics(
         zonal, horizon_tally, quantity_tally, float(lon_total)
     )

time: 120 us -> 127 us (1.058)
  other arithmetic: 18 us -> 22.7 us
  blocking collectives: 42.2 us -> 43.9 us
    psum x1 -> x0, waiting for transfers between devices: 35.3 us -> none  [local(): zonal = lax.psum(partial_value, 'lon')]
    all_gather x0 -> x1, waiting for transfers between devices: none -> 34.8 us  [match_stacks_all_on_mesh(): return jnp.sum(jax.lax.all_gather(incoming_x, a_name), axis=0)]
    concatenate x1, local copies, waits for them, and re-layouts: 0.66 us -> 4.81 us  [local(): jnp.concatenate([jnp.sum(retained_entries * mistake_field * mistake_field...]
    unnamed x14 -> x8, local copies, waits for them, and re-layouts: 7.14 us -> 4.02 us
    reduce_sum x0 -> x1, other arithmetic: none -> 2.66 us  [match_stacks_all_on_mesh(): return jnp.sum(jax.lax.all_gather(incoming_x, a_name), axis=0)]
    reduce_sum x1, other arithmetic: 0.32 us -> 2.38 us  [local(): jnp.sum(retain_filter[None] * observed_anomaly * observed_anomaly, axis=1)]
    psum x1, blocking collectives: 42.2 us -> 43.9 us  [local(): lax.psum(jnp.sum(partial_value * area_factors, axis=1), ('lat', 'lon'))]
  transfers between devices with their start and end apart: 1 -> 1, of which waited for: 1 -> 1; matrix products, arithmetic and copies ran while one was open for 2% -> 5% of each run, Pallas kernels for 0% -> 0%
where the time goes in v1:
time: 127 us
  blocking collectives  43.9 us (35%)
  waiting for transfers between devices  34.9 us (27%)
  other arithmetic  22.7 us (18%)
  between operations  14.2 us (11%)
  local copies, waits for them, and re-layouts  10.8 us (9%)
    psum x1, blocking collectives, local(): lax.psum(jnp.sum(partial_value * area_factors, axis=1), ('lat', 'lon'))  43.9 us
    all_gather x1, waiting for transfers between devices, match_stacks_all_on_mesh(): return jnp.sum(jax.lax.all_gather(incoming_x, a_name), axis=0)  34.8 us
    reduce_sum x1, other arithmetic, local(): jnp.sum(retained_entries * predicted_anomaly * observed_anomaly[None], ax...  10.2 us
    concatenate x1, local copies, waits for them, and re-layouts, local(): jnp.concatenate([jnp.sum(retained_entries * mistake_field * mistake_field...  4.81 us
    unnamed x8, local copies, waits for them, and re-layouts  4.02 us
    reduce_sum x1, other arithmetic, match_stacks_all_on_mesh(): return jnp.sum(jax.lax.all_gather(incoming_x, a_name), axis=0)  2.66 us
  transfers between devices with their start and end apart: 1, of which 1 were waited for; matrix products, arithmetic and copies ran while one was open for 5% of the time, Pallas kernels for 0%

profile of v1, /device:TPU:0, one launch (start us, length us, event | category | flops | bytes accessed | tf_op | source)
XLA Modules:
  0.0 126.5 jit_solution(11009926272718569717)
XLA Ops:
  7.2 0.0 all-gather.4.cloned.1.call-start
  7.2 1.3 %fusion.10 = (s32[]{:T(128)}, s32[]{:T(128)}) fusion(s32[4]{0:T(128)} %param.9, s32[]{:T(128)S(6)} %axis_index.15), kind=kLoop, calls=%fused_computation.33 | loop fusion | flops 22 | bytes 28 | tf_op jit(solution)/shard_map/reduce_sum | solution.py:52
  8.5 0.6 compare_convert_fusion
  9.2 0.0 slice-start
  9.2 1.9 %copy.18 = f32[69,45,128]{2,1,0:T(8,128)S(1)} copy(f32[69,45,128]{2,0,1:T(8,128)} %param.7) | data formatting | bytes 3179520 | tf_op args[2]
  11.1 0.7 convert_multiply_fusion
  11.9 0.0 slice-start.1
  11.9 2.4 %fusion.3 = (f32[69,128]{1,0:T(8,128)S(1)}, f32[69,45,128]{2,0,1:T(8,128)S(1)}) fusion(f32[45,128]{1,0:T(8,128)S(1)} %convert_multiply_fusion, f32[69,45,128]{2,0,1:T(8,128)} %param.6, f32[69,45,128]{2,0,1:T(8,128)} %param.7), kind=kLoop, calls=%fused_computation.8 | loop fusion | flops 1580928 | bytes 4827648 | tf_op jit(solution)/shard_map/reduce_sum | solution.py:80
  14.2 0.3 copy.19
  14.6 0.0 slice-done
  14.6 0.0 slice-done.1
  14.6 10.2 %fusion.1 = (f32[4,69,128]{2,0,1:T(4,128)S(1)}, f32[4,69,128]{2,0,1:T(4,128)S(1)}, f32[4,69,128]{2,0,1:T(4,128)S(1)}, f32[4,69,128]{2,0,1:T(4,128)S(1)}) fusion(f32[4,69,45,128]{3,0,2,1:T(4,128)S(1)} %bitcast.2, f32[69,45,128]{2,1,0:T(8,128)S(1)} %copy.19, f32[69,45,128]{2,1,0:T(8,128)S(1)} %copy.18, f32[45,128]{1,0:T(8,128)S(1)} %convert_multiply_fusion), kind=kLoop, calls=%fused_computation.5 | loop fusion | flops 17346048 | bytes 10126848 | tf_op jit(solution)/shard_map/reduce_sum | solution.py:74
  24.9 4.8 %concatenate.3 = f32[1173,128]{1,0:T(8,128)} concatenate(f32[276,128]{1,0:T(8,128)S(1)} %reshape.153, f32[276,128]{1,0:T(8,128)S(1)} %reshape.154, f32[276,128]{1,0:T(8,128)S(1)} %reshape.155, f32[276,128]{1,0:T(8,128)S(1)} %reshape.156, f32[69,128]{1,0:T(8,128)S(1)} %get-tuple-element.24), dimensions={0} | concatenate | bytes 1201152 | tf_op jit(solution)/shard_map/concatenate | solution.py:68
  29.8 0.0 all-gather.4.cloned.1.call-update
  29.8 0.6 sine_reduce_fusion
  30.4 2.0 %compare_select_fusion.2 = f32[128]{0:T(128)S(1)} fusion(f32[]{:T(128)} %sine_reduce_fusion, s32[]{:T(128)} %get-tuple-element.22, s32[]{:T(128)} %get-tuple-element.23), kind=kLoop, calls=%fused_computation.30 | loop fusion | flops 896 | bytes 524 | tf_op jit(solution)/shard_map/jit(_where)/select_n | solution.py:59
  32.4 1.3 %multiply_reduce_fusion.1 = f32[1173]{0:T(1024)S(1)} fusion(f32[1173,128]{1,0:T(8,128)} %concatenate.3, f32[128]{0:T(128)S(1)} %compare_select_fusion.2), kind=kLoop, calls=%fused_computation.9 | loop fusion | flops 299115 | bytes 605780 | tf_op jit(solution)/shard_map/reduce_sum | solution.py:84
  33.7 43.9 %psum.7 = f32[1173]{0:T(1024)S(1)} all-reduce(f32[1173]{0:T(1024)S(1)} %multiply_reduce_fusion.1), channel_id=1, replica_groups=mesh['lat'=4,'lon'=8] {'lat','lon'}, use_global_device_ids=true, to_apply=%region_10.11 | all-reduce | flops 1173 | bytes 9384 | tf_op jit(solution)/shard_map/psum | solution.py:84
  77.6 0.1 fusion.6
  77.7 0.1 div.94
  77.8 0.1 max.48
  77.9 0.7 div.92
  78.5 0.7 sqrt.14
  79.2 0.1 fusion.11
  79.3 0.6 rsqrt_multiply_fusion.1
  79.9 34.8 %all-gather.4.cloned.1.call-done = f32[8,1173,128]{2,1,0:T(8,128)} async-done(((f32[1,1173,128]{2,1,0:T(8,128)}), f32[8,1173,128]{2,1,0:T(8,128)}) %all-gather.4.cloned.1.call-update) | async-done | bytes 4804624 | tf_op jit(solution)/shard_map/all_gather | solution.py:43
  114.7 2.7 %reduce_sum.96 = f32[1173,128]{1,0:T(8,128)S(1)} reduce(f32[8,1173,128]{2,1,0:T(8,128)} %all-gather.4.cloned.1.call-done, f32[]{:T(128)} %constant.36.clone.1), dimensions={0}, to_apply=%region_6.7 | reduce | flops 1051008 | bytes 5405188 | tf_op jit(solution)/shard_map/reduce_sum | solution.py:43
  117.4 0.1 fusion.4
  117.5 0.7 copy.26
  118.2 0.7 copy.24
  119.0 0.7 copy.25
  (15 shorter events, 0.2 us)
Async XLA Ops:
  7.2 107.5 %all-gather.4.cloned.1.call-start = ((), (), s32[]{:S(2)}) async-start(), calls=%async_computation | async-start | bytes 5419008 | tf_op jit(solution)/shard_map/all_gather | solution.py:43
  9.2 5.4 %slice-start = ((s8[6359040]{0:T(1024)(128)(4,1)}), s8[4194304]{0:T(1024)(128)(4,1)S(1)}, s32[]{:S(2)}) async-start(s8[6359040]{0:T(1024)(128)(4,1)} %bitcast.1), calls=%async_computation.1 | async-start | bytes 8388608
  11.9 2.7 %slice-start.1 = ((s8[6359040]{0:T(1024)(128)(4,1)}), s8[2164736]{0:T(1024)(128)(4,1)S(1)}, s32[]{:S(2)}) async-start(s8[6359040]{0:T(1024)(128)(4,1)} %bitcast.1), calls=%async_computation.2 | async-start | bytes 4329472
Sparse Core Ops, SparseCore 0:
  29.9 84.7 all-gather.3
